TPU v7x, 32 devices: a whole 2x2x4 slice. The times are simulated.
32 devices in a mesh: fsdp: 4 (over y, x), rep: 8 (over z, core).
Axes of the slice: x: 2, y: 2, z: 4, core: 2. Of those that a mesh axis runs over, the one named last changes fastest.
Arguments:
- inputs: bfloat16 [64, 128, 2048], P(('fsdp', 'rep')), may hold values from -6 to 6
- segment_ids: int32 [64, 128], P(('fsdp', 'rep')), may hold values from 0 to 3, never falling along the last dimension, each value on 1 to 64 neighbouring positions
- cotangent: bfloat16 [64, 128, 2048], P(('fsdp', 'rep')), may hold values from -6 to 6
- norm_gain: bfloat16 [2048], replicated, may hold values from 0.5 to 1.5
- norm_shift: bfloat16 [2048], replicated, may hold values from -4 to 4
- qkv_weight: bfloat16 [2048, 6144], P('fsdp'), may hold values from -0.125 to 0.125
- qkv_bias: bfloat16 [6144], replicated, may hold values from -6 to 6
- dense_weight: bfloat16 [2048, 2048], P('fsdp'), may hold values from -0.375 to 0.375
- dense_bias: bfloat16 [2048], replicated, may hold values from -4 to 4
- fc1_weight: bfloat16 [2048, 8192], P('fsdp'), may hold values from -0.125 to 0.125
- fc1_bias: bfloat16 [8192], replicated, may hold values from -6 to 6
- fc2_weight: bfloat16 [8192, 2048], P('fsdp'), may hold values from -0.125 to 0.125
- fc2_bias: bfloat16 [2048], replicated, may hold values from -4 to 4
Outputs:
- layer_output: bfloat16 [64, 128, 2048], P(('fsdp', 'rep'))
- input_grad: bfloat16 [64, 128, 2048], P(('fsdp', 'rep'))
- norm_gain_grad: float32 [2048], P('fsdp')
- norm_shift_grad: float32 [2048], P('fsdp')
- qkv_weight_grad: float32 [2048, 6144], P('fsdp')
- qkv_bias_grad: float32 [6144], P('fsdp')
- dense_weight_grad: float32 [2048, 2048], P('fsdp')
- dense_bias_grad: float32 [2048], P('fsdp')
- fc1_weight_grad: float32 [2048, 8192], P('fsdp')
- fc1_bias_grad: float32 [8192], P('fsdp')
- fc2_weight_grad: float32 [8192, 2048], P('fsdp')
- fc2_bias_grad: float32 [2048], P('fsdp')
Inputs may be any that keep to these rules, and one draw needn't show every extreme that they name: `segment_ids`: along each sequence the document numbers never fall; every document has 1 to 64 tokens, and some document has exactly 64.
All inputs are finite; a program needn't handle non-finite values.
Results may differ from a plain program's by a relative error of at most 0.015.
Values may be sent and summed in bfloat16 or wider, within the bound.
A program may use at most 832 MiB of HBM per device.

v0:
```python
from functools import partial
import jax
import jax.numpy as jnp
from jax import lax
from jax.sharding import PartitionSpec as P

HEADS = 32
HD = 64
ROT = 32
norm_eps = 1e-05


def positions_of(segment_row):
    last_axis = segment_row.ndim - 1
    token_index = lax.broadcasted_iota(jnp.int32, segment_row.shape, last_axis)
    previous = jnp.concatenate([segment_row[..., :1] - 1, segment_row[..., :-1]], axis=last_axis)
    starts = jnp.where(segment_row != previous, token_index, 0)
    return token_index - lax.cummax(starts, axis=last_axis)


def rotary_tables(positions):
    half_rot = ROT // 2
    inv_freq = 10000.0 ** (-2.0 * jnp.arange(half_rot, dtype=jnp.float32) / ROT)
    angles = positions.astype(jnp.float32)[..., None] * inv_freq
    angles = jnp.concatenate([angles, angles], axis=-1)
    return (jnp.cos(angles), jnp.sin(angles))


def rotate(values, cos_tab, sine_tab):
    half_rot = ROT // 2
    turned = values[..., :ROT]
    swapped = jnp.concatenate([-turned[..., half_rot:], turned[..., :half_rot]], axis=-1)
    turned = turned * cos_tab[:, None, :] + swapped * sine_tab[:, None, :]
    return jnp.concatenate([turned, values[..., ROT:]], axis=-1)


def rotate_back(grad_in, cos_tab, sine_tab):
    half_rot = ROT // 2
    rot_part = grad_in[..., :ROT]
    scaled = rot_part * sine_tab[:, None, :]
    rot_back = jnp.concatenate([scaled[..., half_rot:], -scaled[..., :half_rot]], axis=-1)
    rot_part = rot_part * cos_tab[:, None, :] + rot_back
    return jnp.concatenate([rot_part, grad_in[..., ROT:]], axis=-1)


def dot_last(left_op, right_op):
    return lax.dot_general(
        left_op, right_op, (((1,), (1,)), ((), ())), preferred_element_type=jnp.float32
    )


def dot_first(left_op, right_op):
    return lax.dot_general(
        left_op, right_op, (((0,), (0,)), ((), ())), preferred_element_type=jnp.float32
    )


def row_adder(left_b):

    def add_rows(running, shard_rows, first_row):
        return jnp.dot(left_b, shard_rows, preferred_element_type=jnp.float32)

    return add_rows


def column_maker(back_b, shard_rows):
    return dot_last(back_b, shard_rows)


def gelu_back(pre_act, d_hidden):
    gelu_vals, pull_back = jax.vjp(partial(jax.nn.gelu, approximate=True), pre_act)
    return pull_back(d_hidden)[0]


def per_device(
    inputs,
    segment_ids,
    cotangent,
    norm_gain,
    norm_shift,
    qkv_weight,
    qkv_bias,
    dense_weight,
    dense_bias,
    fc1_weight,
    fc1_bias,
    fc2_weight,
    fc2_bias,
):
    micro_count, seq_len, model_width = inputs.shape
    ffn_width = fc1_weight.shape[1]
    score_scale = HD ** (-0.5)
    gain_f32 = norm_gain.astype(jnp.float32)
    shift_f32 = norm_shift.astype(jnp.float32)
    qkv_bias_f32 = qkv_bias.astype(jnp.float32)
    dense_bias_f32 = dense_bias.astype(jnp.float32)
    fc1_bias_f32 = fc1_bias.astype(jnp.float32)
    fc2_bias_f32 = fc2_bias.astype(jnp.float32)
    token_index = jnp.arange(seq_len, dtype=jnp.int32)
    causal = token_index[:, None] >= token_index[None, :]
    layer_outs = []
    input_grads = []
    kept_normed = []
    kept_joined = []
    kept_pre = []
    kept_mixed = []
    kept_hidden = []
    kept_back = []
    gain_sum = jnp.zeros((model_width,), jnp.float32)
    shift_sum = jnp.zeros((model_width,), jnp.float32)
    qkv_bias_sum = jnp.zeros((3 * model_width,), jnp.float32)
    back_sum = jnp.zeros((model_width,), jnp.float32)
    fc1_bias_sum = jnp.zeros((ffn_width,), jnp.float32)
    for micro_step in range(micro_count):
        token_rows = inputs[micro_step].astype(jnp.float32)
        segment_row = segment_ids[micro_step]
        row_mean = jnp.mean(token_rows, axis=-1, keepdims=True)
        centred = token_rows - row_mean
        row_var = jnp.mean(centred * centred, axis=-1, keepdims=True)
        inv_std = lax.rsqrt(row_var + norm_eps)
        x_hat = centred * inv_std
        normed = (x_hat * gain_f32 + shift_f32).astype(jnp.bfloat16)
        add_normed = row_adder(normed)
        start_sums = (
            jnp.zeros((seq_len, 3 * model_width), jnp.float32),
            jnp.zeros((seq_len, ffn_width), jnp.float32),
        )
        add_first_row = jnp.int32(0)
        joined_qkv = add_normed(
            start_sums[0], lax.all_gather(qkv_weight, "fsdp", axis=0, tiled=True), add_first_row
        )
        pre_act = add_normed(
            start_sums[1], lax.all_gather(fc1_weight, "fsdp", axis=0, tiled=True), add_first_row
        )
        joined_qkv = joined_qkv + qkv_bias_f32
        pre_act = pre_act + fc1_bias_f32
        hidden_b = jax.nn.gelu(pre_act, approximate=True).astype(jnp.bfloat16)
        cos_tab, sine_tab = rotary_tables(positions_of(segment_row))
        joined_heads = joined_qkv.reshape(seq_len, 3, HEADS, HD)
        query_b = rotate(joined_heads[:, 0], cos_tab, sine_tab).astype(jnp.bfloat16)
        key_b = rotate(joined_heads[:, 1], cos_tab, sine_tab).astype(jnp.bfloat16)
        value_b = joined_heads[:, 2].astype(jnp.bfloat16)
        allowed = causal & (segment_row[:, None] == segment_row[None, :])
        scores = (
            jnp.einsum("qhd,khd->hqk", query_b, key_b, preferred_element_type=jnp.float32)
            * score_scale
        )
        scores = jnp.where(allowed[None], scores, -1e30)
        row_max = jnp.max(scores, axis=-1, keepdims=True)
        exp_scores = jnp.exp(scores - row_max)
        row_total = jnp.sum(exp_scores, axis=-1, keepdims=True)
        probs_b = (exp_scores / row_total).astype(jnp.bfloat16)
        log_total = row_max + jnp.log(row_total)
        mixed_b = jnp.einsum("hqk,khd->qhd", probs_b, value_b, preferred_element_type=jnp.float32)
        mixed_b = mixed_b.reshape(seq_len, model_width).astype(jnp.bfloat16)
        start_out = jnp.zeros((seq_len, model_width), jnp.float32)
        attn_out = row_adder(mixed_b)(
            start_out, lax.all_gather(dense_weight, "fsdp", axis=0, tiled=True), jnp.int32(0)
        )
        mlp_out = row_adder(hidden_b)(
            start_out, lax.all_gather(fc2_weight, "fsdp", axis=0, tiled=True), jnp.int32(0)
        )
        layer_outs.append(
            (token_rows + attn_out + dense_bias_f32 + mlp_out + fc2_bias_f32).astype(jnp.bfloat16)
        )
        back_b = cotangent[micro_step]
        back_f32 = back_b.astype(jnp.float32)
        back_sum = back_sum + jnp.sum(back_f32, axis=0)
        d_mixed = column_maker(back_b, lax.all_gather(dense_weight, "fsdp", axis=0, tiled=True))
        d_hidden = column_maker(back_b, lax.all_gather(fc2_weight, "fsdp", axis=0, tiled=True))
        d_mixed_b = d_mixed.astype(jnp.bfloat16).reshape(seq_len, HEADS, HD)
        d_pre_b = gelu_back(pre_act, d_hidden).astype(jnp.bfloat16)
        fc1_bias_sum = fc1_bias_sum + jnp.sum(d_pre_b, axis=0, dtype=jnp.float32)
        again_scores = (
            jnp.einsum("qhd,khd->hqk", query_b, key_b, preferred_element_type=jnp.float32)
            * score_scale
        )
        again_scores = jnp.where(allowed[None], again_scores, -1e30)
        attn_probs = jnp.exp(again_scores - log_total)
        d_probs = jnp.einsum("qhd,khd->hqk", d_mixed_b, value_b, preferred_element_type=jnp.float32)
        d_value = jnp.einsum(
            "hqk,qhd->khd",
            attn_probs.astype(jnp.bfloat16),
            d_mixed_b,
            preferred_element_type=jnp.float32,
        )
        d_scores_b = (
            attn_probs * (d_probs - jnp.sum(attn_probs * d_probs, axis=-1, keepdims=True))
        ).astype(jnp.bfloat16)
        d_query = (
            jnp.einsum("hqk,khd->qhd", d_scores_b, key_b, preferred_element_type=jnp.float32)
            * score_scale
        )
        d_key = (
            jnp.einsum("hqk,qhd->khd", d_scores_b, query_b, preferred_element_type=jnp.float32)
            * score_scale
        )
        d_query = rotate_back(d_query, cos_tab, sine_tab)
        d_key = rotate_back(d_key, cos_tab, sine_tab)
        d_joined_b = (
            jnp.stack([d_query, d_key, d_value], axis=1)
            .reshape(seq_len, 3 * model_width)
            .astype(jnp.bfloat16)
        )
        qkv_bias_sum = qkv_bias_sum + jnp.sum(d_joined_b, axis=0, dtype=jnp.float32)
        block_cols = dot_last(
            d_joined_b, lax.all_gather(qkv_weight, "fsdp", axis=0, tiled=True)
        ) + dot_last(d_pre_b, lax.all_gather(fc1_weight, "fsdp", axis=0, tiled=True))
        gain_sum = gain_sum + jnp.sum(block_cols * x_hat, axis=0)
        shift_sum = shift_sum + jnp.sum(block_cols, axis=0)
        d_hat = block_cols * gain_f32
        d_input = inv_std * (
            d_hat
            - jnp.mean(d_hat, axis=-1, keepdims=True)
            - x_hat * jnp.mean(d_hat * x_hat, axis=-1, keepdims=True)
        )
        input_grads.append((back_f32 + d_input).astype(jnp.bfloat16))
        kept_normed.append(normed)
        kept_joined.append(d_joined_b)
        kept_pre.append(d_pre_b)
        kept_mixed.append(mixed_b)
        kept_hidden.append(hidden_b)
        kept_back.append(back_b)
    normed_all = jnp.concatenate(kept_normed, axis=0)
    joined_all = jnp.concatenate(kept_joined, axis=0)
    pre_all = jnp.concatenate(kept_pre, axis=0)
    mixed_all = jnp.concatenate(kept_mixed, axis=0)
    hidden_all = jnp.concatenate(kept_hidden, axis=0)
    back_all = jnp.concatenate(kept_back, axis=0)
    dense_rows = dense_weight.shape[0]
    fc2_rows = fc2_weight.shape[0]
    block_rows = dense_rows + fc2_rows
    first_rows = lax.psum_scatter(
        jnp.concatenate(
            [dot_first(normed_all, joined_all), dot_first(normed_all, pre_all)], axis=1
        ).astype(jnp.bfloat16),
        "fsdp",
        scatter_dimension=0,
        tiled=True,
    )
    first_row = jnp.int32(0)
    collected = []
    for offset in range(block_rows * lax.axis_size("fsdp") // block_rows):
        owner_idx = first_row // block_rows + offset
        mixed_cols = lax.dynamic_slice_in_dim(mixed_all, owner_idx * dense_rows, dense_rows, 1)
        hid_cols = lax.dynamic_slice_in_dim(hidden_all, owner_idx * fc2_rows, fc2_rows, 1)
        collected.append(dot_first(mixed_cols, back_all))
        collected.append(dot_first(hid_cols, back_all))
    second_rows = lax.psum_scatter(
        jnp.concatenate(collected, axis=0).astype(jnp.bfloat16),
        "fsdp",
        scatter_dimension=0,
        tiled=True,
    )
    small_sums = (
        lax.psum_scatter(
            gain_sum.astype(jnp.bfloat16), "fsdp", scatter_dimension=0, tiled=True
        ).astype(jnp.float32),
        lax.psum_scatter(
            shift_sum.astype(jnp.bfloat16), "fsdp", scatter_dimension=0, tiled=True
        ).astype(jnp.float32),
        lax.psum_scatter(
            qkv_bias_sum.astype(jnp.bfloat16), "fsdp", scatter_dimension=0, tiled=True
        ).astype(jnp.float32),
        lax.psum_scatter(
            back_sum.astype(jnp.bfloat16), "fsdp", scatter_dimension=0, tiled=True
        ).astype(jnp.float32),
        lax.psum_scatter(
            fc1_bias_sum.astype(jnp.bfloat16), "fsdp", scatter_dimension=0, tiled=True
        ).astype(jnp.float32),
    )
    totals = (
        lax.psum(first_rows, "rep").astype(jnp.float32),
        lax.psum(second_rows, "rep").astype(jnp.float32),
        lax.psum(small_sums[0].astype(jnp.bfloat16), "rep").astype(jnp.float32),
        lax.psum(small_sums[1].astype(jnp.bfloat16), "rep").astype(jnp.float32),
        lax.psum(small_sums[2].astype(jnp.bfloat16), "rep").astype(jnp.float32),
        lax.psum(small_sums[3].astype(jnp.bfloat16), "rep").astype(jnp.float32),
        lax.psum(small_sums[4].astype(jnp.bfloat16), "rep").astype(jnp.float32),
    )
    first_total = totals[0]
    second_total = totals[1]
    return (
        jnp.stack(layer_outs, axis=0),
        jnp.stack(input_grads, axis=0),
        totals[2],
        totals[3],
        first_total[:, : 3 * model_width],
        totals[4],
        second_total[:dense_rows],
        totals[5],
        first_total[:, 3 * model_width :],
        totals[6],
        second_total[dense_rows:],
        totals[5],
    )


def solution(mesh):
    placed = (
        P(("fsdp", "rep"), None, None),
        P(("fsdp", "rep"), None),
        P(("fsdp", "rep"), None, None),
        P(),
        P(),
        P("fsdp", None),
        P(),
        P("fsdp", None),
        P(),
        P("fsdp", None),
        P(),
        P("fsdp", None),
        P(),
    )
    return jax.shard_map(
        per_device,
        mesh=mesh,
        in_specs=placed,
        out_specs=(
            P(("fsdp", "rep"), None, None),
            P(("fsdp", "rep"), None, None),
            P("fsdp"),
            P("fsdp"),
            P("fsdp", None),
            P("fsdp"),
            P("fsdp", None),
            P("fsdp"),
            P("fsdp", None),
            P("fsdp"),
            P("fsdp", None),
            P("fsdp"),
        ),
        check_vma=False,
    )
```

profile of v0, /device:TPU:0, one launch (start us, length us, event | category | flops | bytes accessed | tf_op | source)
XLA Modules:
  0.0 2319.4 jit_solution(13919648007534341312)
XLA Ops:
  17.1 223.1 %all-gather.5.cloned.1.call-done = bf16[2048,6144]{1,0:T(8,128)(2,1)} async-done(((bf16[512,6144]{1,0:T(8,128)(2,1)}), bf16[2048,6144]{1,0:T(8,128)(2,1)}) %all-gather.5.cloned.1.call-update) | async-done | bytes 25165840 | tf_op jit(solution)/shard_map/all_gather | solution.py:130
  240.2 10.5 convolution_add_fusion.3
  257.7 13.4 convolution_add_fusion.2
  285.0 254.1 %all-gather.9.cloned.1.call-done = bf16[2048,8192]{1,0:T(8,128)(2,1)} async-done(((bf16[512,8192]{1,0:T(8,128)(2,1)}), bf16[2048,8192]{1,0:T(8,128)(2,1)}) %all-gather.9.cloned.1.call-update) | async-done | bytes 33554448 | tf_op jit(solution)/shard_map/all_gather | solution.py:133
  539.1 17.8 multiply_convert_fusion.1
  557.0 16.7 multiply_convert_fusion
  596.9 5.7 convert_dynamic-update-slice_fusion
  602.9 25.6 %all-gather.7.cloned.1.call-done = bf16[2048,2048]{1,0:T(8,128)(2,1)} async-done(((bf16[512,2048]{1,0:T(8,128)(2,1)}), bf16[2048,2048]{1,0:T(8,128)(2,1)}) %all-gather.7.cloned.1.call-update) | async-done | bytes 8388624 | tf_op jit(solution)/shard_map/all_gather | solution.py:158
  628.5 7.1 convolution_convert_fusion.6
  637.7 10.0 convolution_convert_fusion.7
  664.6 13.2 convolution_convert_fusion.1
  677.8 249.5 %all-gather.11.cloned.1.call-done = bf16[8192,2048]{1,0:T(8,128)(2,1)} async-done(((bf16[2048,2048]{1,0:T(8,128)(2,1)}), bf16[8192,2048]{1,0:T(8,128)(2,1)}) %all-gather.11.cloned.1.call-update) | async-done | bytes 33554448 | tf_op jit(solution)/shard_map/all_gather | solution.py:161
  927.3 19.3 convert_reduce_fusion.1
  946.6 19.7 convert_reduce_fusion
  966.3 17.0 convolution_convert_fusion
  983.3 40.6 %pad_maximum_fusion = bf16[2048,14336]{1,0:T(8,128)(2,1)} fusion(bf16[2048,8192]{1,0:T(8,128)(2,1)} %convolution_convert_fusion, bf16[2048,6144]{1,0:T(8,128)(2,1)} %convolution_convert_fusion.1), kind=kLoop, calls=%fused_computation | loop fusion | flops 117440512 | bytes 117440512 | tf_op jit(solution)/shard_map/concatenate | solution.py:234
  1027.3 6.0 fusion.26
  1033.4 6.0 fusion.27
  1039.4 14.7 fusion.137
  1054.0 232.5 %reduce-scatter.7.cloned.1.call-done = bf16[2560,2048]{1,0:T(8,128)(2,1)} async-done(((bf16[10240,2048]{1,0:T(8,128)(2,1)}), bf16[2560,2048]{1,0:T(8,128)(2,1)}) %reduce-scatter.7.cloned.1.call-update) | async-done | bytes 10485776
  1286.6 494.7 %reduce-scatter.5.cloned.1.call-done = bf16[512,14336]{1,0:T(8,128)(2,1)} async-done(((bf16[2048,14336]{1,0:T(8,128)(2,1)}), bf16[512,14336]{1,0:T(8,128)(2,1)}) %reduce-scatter.5.cloned.1.call-update) | async-done | bytes 14680080 | tf_op jit(solution)/shard_map/reduce_scatter | solution.py:233
  1781.2 14.2 fusion.138
  1795.4 17.0 convolution_add_fusion.4
  1812.5 19.8 fusion.66
  1835.7 15.9 all-reduce.8
  1851.9 27.9 %all-reduce.6 = (bf16[512]{0:T(512)(128)(2,1)S(1)}, bf16[512]{0:T(512)(128)(2,1)S(1)}, bf16[1536]{0:T(1024)(128)(2,1)S(1)}, bf16[512]{0:T(512)(128)(2,1)S(1)}, bf16[2048]{0:T(1024)(128)(2,1)S(1)}) all-reduce(bf16[512]{0:T(512)(128)(2,1)S(1)} %dynamic-slice.1, ...), channel_id=1, replica_groups=mesh['fsdp'=4,'rep'=8] {'rep'}, use_global_device_ids=true, to_apply=%region_19.20 | all-reduce | flops 5120 | bytes 20480 | tf_op jit(solution)/shard_map/psum | solution.py:275
  1882.2 16.4 fusion.31
  1898.6 14.2 fusion.30
  1914.9 360.0 %all-reduce.11.cloned.1.call-done = (bf16[512,14336]{1,0:T(8,128)(2,1)}, bf16[2560,2048]{1,0:T(8,128)(2,1)}) async-done(((bf16[512,14336]{1,0:T(8,128)(2,1)}, bf16[2560,2048]{1,0:T(8,128)(2,1)}), (bf16[512,14336]{1,0:T(8,128)(2,1)}, bf16[2560,2048]{1,0:T(8,128)(2,1)})) %all-reduce.11.cloned.1.call-update) | async-done | bytes 25165840 | tf_op jit(solution)/shard_map/psum | solution.py:273
  2279.1 11.7 slice.279
  2290.8 9.2 slice.276
  2300.0 11.7 slice.278
  (258 shorter events, 85.4 us)
Async XLA Ops:
  7.2 233.0 %all-gather.5.cloned.1.call-start = ((), (), s32[]{:S(2)}) async-start(), calls=%async_computation.2 | async-start | bytes 31457280 | tf_op jit(solution)/shard_map/all_gather | solution.py:130
  7.9 531.2 %all-gather.9.cloned.1.call-start = ((), (), s32[]{:S(2)}) async-start(), calls=%async_computation.4 | async-start | bytes 41943040 | tf_op jit(solution)/shard_map/all_gather | solution.py:133
  8.7 619.8 %all-gather.7.cloned.1.call-start = ((), (), s32[]{:S(2)}) async-start(), calls=%async_computation.3 | async-start | bytes 10485760 | tf_op jit(solution)/shard_map/all_gather | solution.py:158
  9.5 917.8 %all-gather.11.cloned.1.call-start = ((), (), s32[]{:S(2)}) async-start(), calls=%async_computation.5 | async-start | bytes 41943040 | tf_op jit(solution)/shard_map/all_gather | solution.py:161
  10.0 1276.5 %reduce-scatter.7.cloned.1.call-start = ((), (), s32[]{:S(2)}) async-start(), calls=%async_computation.7 | async-start | bytes 52428800
  12.0 238.7 %copy-start.47 = (f32[2048]{0:T(1024)}, f32[2048]{0:T(1024)S(1)}, u32[]{:S(2)}) copy-start(f32[2048]{0:T(1024)S(1)} %convert_element_type.215) | copy-start | bytes 24580
  13.9 236.8 %copy-start.52 = (f32[128]{0:T(128)}, f32[128]{0:T(128)S(1)}, u32[]{:S(2)}) copy-start(f32[128]{0:T(128)S(1)} %get-tuple-element.123) | copy-start | bytes 1540
  13.9 236.8 %copy-start.54 = (f32[128]{0:T(128)}, f32[128]{0:T(128)S(1)}, u32[]{:S(2)}) copy-start(f32[128]{0:T(128)S(1)} %get-tuple-element.124) | copy-start | bytes 1540
  14.4 236.3 %copy-start.58 = (f32[128]{0:T(128)}, f32[128]{0:T(128)S(1)}, u32[]{:S(2)}) copy-start(f32[128]{0:T(128)S(1)} %add_rsqrt_fusion.1) | copy-start | bytes 1540
  14.4 236.3 %copy-start.60 = (f32[128]{0:T(128)}, f32[128]{0:T(128)S(1)}, u32[]{:S(2)}) copy-start(f32[128]{0:T(128)S(1)} %add_rsqrt_fusion) | copy-start | bytes 1540
  282.2 257.0 %copy-start.8 = (bf16[128,2048]{1,0:T(8,128)(2,1)S(1)}, bf16[128,2048]{1,0:T(8,128)(2,1)}, u32[]{:S(2)}) copy-start(bf16[128,2048]{1,0:T(8,128)(2,1)} %get-tuple-element.50) | copy-start | bytes 1572868
  285.0 271.9 %copy-start.11 = (bf16[128,2048]{1,0:T(8,128)(2,1)S(1)}, bf16[128,2048]{1,0:T(8,128)(2,1)}, u32[]{:S(2)}) copy-start(bf16[128,2048]{1,0:T(8,128)(2,1)} %get-tuple-element.51) | copy-start | bytes 1572868
  539.1 17.8 copy-start.49
  557.0 40.0 %copy-start.20 = (bf16[128,8192]{1,0:T(8,128)(2,1)}, bf16[128,8192]{1,0:T(8,128)(2,1)S(1)}, u32[]{:S(2)}) copy-start(bf16[128,8192]{1,0:T(8,128)(2,1)S(1)} %get-tuple-element.112) | copy-start | bytes 6291460
  557.0 16.7 copy-start.44
  557.0 16.7 copy-start.46
  573.7 23.2 %copy-start.18 = (bf16[128,8192]{1,0:T(8,128)(2,1)}, bf16[128,8192]{1,0:T(8,128)(2,1)S(1)}, u32[]{:S(2)}) copy-start(bf16[128,8192]{1,0:T(8,128)(2,1)S(1)} %get-tuple-element.108) | copy-start | bytes 6291460
  602.6 25.9 %copy-start.5 = (bf16[2,128,2048]{2,1,0:T(8,128)(2,1)S(1)}, bf16[2,128,2048]{2,1,0:T(8,128)(2,1)}, u32[]{:S(2)}) copy-start(bf16[2,128,2048]{2,1,0:T(8,128)(2,1)} %param.15) | copy-start | bytes 3145732
  602.7 1178.6 %reduce-scatter.5.cloned.1.call-start = ((), (), s32[]{:S(2)}) async-start(), calls=%async_computation.6 | async-start | bytes 73400320 | tf_op jit(solution)/shard_map/reduce_scatter | solution.py:233
  664.6 262.7 %copy-start.6 = (bf16[2,128,2048]{2,1,0:T(8,128)(2,1)S(1)}, bf16[2,128,2048]{2,1,0:T(8,128)(2,1)}, u32[]{:S(2)}) copy-start(bf16[2,128,2048]{2,1,0:T(8,128)(2,1)} %param.15) | copy-start | bytes 3145732
  1024.1 1250.9 %all-reduce.11.cloned.1.call-start = ((), (), s32[]{:S(2)}) async-start(), calls=%async_computation.8 | async-start | bytes 50331648 | tf_op jit(solution)/shard_map/psum | solution.py:273
  1795.4 17.0 copy-start.48
  1795.4 17.0 copy-start.53
  1795.4 17.0 copy-start.55
  1795.4 17.0 copy-start.59
  1795.4 17.0 copy-start.61
  1812.5 19.8 copy-start.7
  1880.4 431.4 %copy-start.57 = (f32[512]{0:T(512)}, f32[512]{0:T(512)S(1)}, u32[]{:S(2)}) copy-start(f32[512]{0:T(512)S(1)} %convert_element_type.269) | copy-start | bytes 6148
  1882.2 16.4 copy-start.17
  1882.2 16.4 copy-start.19
  1898.6 15.3 copy-start.21
  1898.6 15.3 copy-start.22
  (42 other events, 111.3 us)
Sparse Core Ops, SparseCore 0:
  9.9 230.2 all-gather.4
  242.0 297.0 all-gather.8
  541.0 87.4 all-gather.6
  630.2 297.0 all-gather.10
  930.3 356.2 reduce-scatter.6
  1289.5 491.6 reduce-scatter.4
  1783.8 491.0 all-reduce.10
where the time goes:
time: 2320 us
  waiting for transfers between devices  1840 us (79%)
  matrix products  297 us (13%)
  other arithmetic  59.1 us (3%)
  local copies, waits for them, and re-layouts  57.9 us (2%)
  blocking collectives  43.8 us (2%)
    reduce_scatter x1, waiting for transfers between devices, per_device(): lax.psum_scatter(jnp.concatenate([dot_first(normed_all, joined_all), dot_...  495 us
    psum x1, waiting for transfers between devices, per_device(): lax.psum(first_rows, 'rep').astype(jnp.float32)  360 us
    all_gather x1, waiting for transfers between devices, per_device(): lax.all_gather(fc1_weight, 'fsdp', axis=0, tiled=True)  254 us
    all_gather x1, waiting for transfers between devices, per_device(): lax.all_gather(fc2_weight, 'fsdp', axis=0, tiled=True)  249 us
    unnamed x8, waiting for transfers between devices  235 us
    all_gather x1, waiting for transfers between devices, per_device(): lax.all_gather(qkv_weight, 'fsdp', axis=0, tiled=True)  223 us
    dot_general x8, matrix products, dot_last(): lax.dot_general(left_op, right_op, (((1,), (1,)), ((), ())), preferred_el...  122 us
    dot_general x8, matrix products, add_rows(): return jnp.dot(left_b, shard_rows, preferred_element_type=jnp.float32)  101 us
  transfers between devices with their start and end apart: 7, of which 7 were waited for; matrix products, arithmetic and copies ran while one was open for 16% of the time, Pallas kernels for 0%

commit v1 on v0

--- a/solution.py
+++ b/solution.py
@@ -270,7 +270,7 @@
         ).astype(jnp.float32),
     )
     totals = (
-        lax.psum(first_rows, "rep").astype(jnp.float32),
+        jnp.sum(lax.all_gather(first_rows, "rep"), axis=0).astype(jnp.float32),
         lax.psum(second_rows, "rep").astype(jnp.float32),
         lax.psum(small_sums[0].astype(jnp.bfloat16), "rep").astype(jnp.float32),
         lax.psum(small_sums[1].astype(jnp.bfloat16), "rep").astype(jnp.float32),

time: 2320 us -> 3060 us (1.32)
  waiting for transfers between devices: 1840 us -> 2530 us
  other arithmetic: 59.1 us -> 103 us
    all_gather x0 -> x1, waiting for transfers between devices: none -> 958 us  [per_device(): lax.all_gather(first_rows, 'rep')]
    psum x1, waiting for transfers between devices: 360 us -> 55.2 us  [per_device(): lax.psum(second_rows, 'rep').astype(jnp.float32)]
    reduce_sum x0 -> x1, other arithmetic: none -> 44.4 us  [per_device(): jnp.sum(lax.all_gather(first_rows, 'rep'), axis=0).astype(jnp.float32)]
    unnamed x8 -> x9, waiting for transfers between devices: 235 us -> 265 us
  transfers between devices with their start and end apart: 7 -> 8, of which waited for: 7 -> 8; matrix products, arithmetic and copies ran while one was open for 16% -> 13% of each run, Pallas kernels for 0% -> 0%
where the time goes in v1:
time: 3060 us; the launch traced here: 3050 us
  waiting for transfers between devices  2530 us (83%)
  matrix products  297 us (10%)
  other arithmetic  103 us (3%)
  local copies, waits for them, and re-layouts  64.3 us (2%)
  blocking collectives  43.2 us (1%)
    all_gather x1, waiting for transfers between devices, per_device(): lax.all_gather(first_rows, 'rep')  958 us
    reduce_scatter x1, waiting for transfers between devices, per_device(): lax.psum_scatter(jnp.concatenate([dot_first(normed_all, joined_all), dot_...  495 us
    unnamed x9, waiting for transfers between devices  265 us
    all_gather x1, waiting for transfers between devices, per_device(): lax.all_gather(fc1_weight, 'fsdp', axis=0, tiled=True)  254 us
    all_gather x1, waiting for transfers between devices, per_device(): lax.all_gather(fc2_weight, 'fsdp', axis=0, tiled=True)  249 us
    all_gather x1, waiting for transfers between devices, per_device(): lax.all_gather(qkv_weight, 'fsdp', axis=0, tiled=True)  223 us
    dot_general x8, matrix products, dot_last(): lax.dot_general(left_op, right_op, (((1,), (1,)), ((), ())), preferred_el...  123 us
    dot_general x8, matrix products, add_rows(): return jnp.dot(left_b, shard_rows, preferred_element_type=jnp.float32)  99.4 us
  transfers between devices with their start and end apart: 8, of which 8 were waited for; matrix products, arithmetic and copies ran while one was open for 13% of the time, Pallas kernels for 0%

profile of v1, /device:TPU:0, one launch (start us, length us, event | category | flops | bytes accessed | tf_op | source)
XLA Modules:
  0.0 3052.0 jit_solution(5457248925414671754)
XLA Ops:
  17.0 223.1 %all-gather.7.cloned.1.call-done = bf16[2048,6144]{1,0:T(8,128)(2,1)} async-done(((bf16[512,6144]{1,0:T(8,128)(2,1)}), bf16[2048,6144]{1,0:T(8,128)(2,1)}) %all-gather.7.cloned.1.call-update) | async-done | bytes 25165840 | tf_op jit(solution)/shard_map/all_gather | solution.py:130
  240.2 10.5 convolution_add_fusion.2
  257.8 13.4 convolution_add_fusion.3
  285.0 254.1 %all-gather.11.cloned.1.call-done = bf16[2048,8192]{1,0:T(8,128)(2,1)} async-done(((bf16[512,8192]{1,0:T(8,128)(2,1)}), bf16[2048,8192]{1,0:T(8,128)(2,1)}) %all-gather.11.cloned.1.call-update) | async-done | bytes 33554448 | tf_op jit(solution)/shard_map/all_gather | solution.py:133
  539.1 17.6 multiply_convert_fusion
  556.8 16.7 multiply_convert_fusion.1
  596.6 5.7 convert_dynamic-update-slice_fusion
  602.6 26.0 all-gather.9.cloned.1.call-done
  628.6 7.1 convolution_convert_fusion.6
  637.8 10.0 convolution_convert_fusion.7
  665.5 13.2 convolution_convert_fusion.1
  678.7 248.7 %all-gather.13.cloned.1.call-done = bf16[8192,2048]{1,0:T(8,128)(2,1)} async-done(((bf16[2048,2048]{1,0:T(8,128)(2,1)}), bf16[8192,2048]{1,0:T(8,128)(2,1)}) %all-gather.13.cloned.1.call-update) | async-done | bytes 33554448 | tf_op jit(solution)/shard_map/all_gather | solution.py:161
  927.4 19.3 convert_reduce_fusion
  946.6 19.7 convert_reduce_fusion.1
  966.4 17.0 convolution_convert_fusion
  983.4 40.6 %pad_maximum_fusion = bf16[2048,14336]{1,0:T(8,128)(2,1)} fusion(bf16[2048,8192]{1,0:T(8,128)(2,1)} %convolution_convert_fusion, bf16[2048,6144]{1,0:T(8,128)(2,1)} %convolution_convert_fusion.1), kind=kLoop, calls=%fused_computation | loop fusion | flops 117440512 | bytes 117440512 | tf_op jit(solution)/shard_map/concatenate | solution.py:234
  1024.1 262.5 %reduce-scatter.7.cloned.1.call-done = bf16[2560,2048]{1,0:T(8,128)(2,1)} async-done(((bf16[10240,2048]{1,0:T(8,128)(2,1)}), bf16[2560,2048]{1,0:T(8,128)(2,1)}) %reduce-scatter.7.cloned.1.call-update) | async-done | bytes 10485776
  1286.7 494.6 %reduce-scatter.5.cloned.1.call-done = bf16[512,14336]{1,0:T(8,128)(2,1)} async-done(((bf16[2048,14336]{1,0:T(8,128)(2,1)}), bf16[512,14336]{1,0:T(8,128)(2,1)}) %reduce-scatter.5.cloned.1.call-update) | async-done | bytes 14680080 | tf_op jit(solution)/shard_map/reduce_scatter | solution.py:233
  1796.0 14.5 fusion.138
  1810.5 14.5 fusion.137
  1825.0 17.5 convolution_add_fusion.4
  1842.6 19.9 fusion.66
  1866.0 16.1 all-reduce.7
  1882.4 27.1 all-reduce.6
  1911.8 16.4 fusion.30
  1928.3 13.5 fusion.31
  1943.9 55.2 %all-reduce.10.cloned.1.call-done = bf16[2560,2048]{1,0:T(8,128)(2,1)} async-done(((bf16[2560,2048]{1,0:T(8,128)(2,1)}), bf16[2560,2048]{1,0:T(8,128)(2,1)}) %all-reduce.10.cloned.1.call-update) | async-done | bytes 10485776 | tf_op jit(solution)/shard_map/psum | solution.py:274
  2003.3 17.6 slice.279
  2020.8 958.1 %all-gather.15.cloned.1.call-done = bf16[4096,14336]{1,0:T(8,128)(2,1)} async-done(((bf16[512,14336]{1,0:T(8,128)(2,1)}), bf16[4096,14336]{1,0:T(8,128)(2,1)}) %all-gather.15.cloned.1.call-update) | async-done | bytes 117440528 | tf_op jit(solution)/shard_map/all_gather | solution.py:273
  2978.9 44.4 %reduce_sum.226 = bf16[512,14336]{1,0:T(8,128)(2,1)} reduce(bf16[8,512,14336]{2,1,0:T(8,128)(2,1)} %bitcast.42, bf16[]{:T(256)} %constant.116.clone.1), dimensions={0}, to_apply=%region_25.26 | reduce | flops 51380224 | bytes 132120576 | tf_op jit(solution)/shard_map/reduce_sum | solution.py:273
  3023.3 9.2 slice.276
  3032.6 11.7 slice.278
  (270 shorter events, 97.5 us)
Async XLA Ops:
  7.2 233.0 %all-gather.7.cloned.1.call-start = ((), (), s32[]{:S(2)}) async-start(), calls=%async_computation.2 | async-start | bytes 31457280 | tf_op jit(solution)/shard_map/all_gather | solution.py:130
  7.9 531.2 %all-gather.11.cloned.1.call-start = ((), (), s32[]{:S(2)}) async-start(), calls=%async_computation.4 | async-start | bytes 41943040 | tf_op jit(solution)/shard_map/all_gather | solution.py:133
  8.7 619.9 %all-gather.9.cloned.1.call-start = ((), (), s32[]{:S(2)}) async-start(), calls=%async_computation.3 | async-start | bytes 10485760 | tf_op jit(solution)/shard_map/all_gather | solution.py:158
  9.5 917.9 %all-gather.13.cloned.1.call-start = ((), (), s32[]{:S(2)}) async-start(), calls=%async_computation.5 | async-start | bytes 41943040 | tf_op jit(solution)/shard_map/all_gather | solution.py:161
  10.0 1276.6 %reduce-scatter.7.cloned.1.call-start = ((), (), s32[]{:S(2)}) async-start(), calls=%async_computation.9 | async-start | bytes 52428800
  10.1 240.6 %copy-start.51 = (f32[2048]{0:T(1024)}, f32[2048]{0:T(1024)S(1)}, u32[]{:S(2)}) copy-start(f32[2048]{0:T(1024)S(1)} %convert_element_type.217) | copy-start | bytes 24580
  13.9 236.8 %copy-start.56 = (f32[128]{0:T(128)}, f32[128]{0:T(128)S(1)}, u32[]{:S(2)}) copy-start(f32[128]{0:T(128)S(1)} %get-tuple-element.121) | copy-start | bytes 1540
  13.9 236.8 %copy-start.58 = (f32[128]{0:T(128)}, f32[128]{0:T(128)S(1)}, u32[]{:S(2)}) copy-start(f32[128]{0:T(128)S(1)} %get-tuple-element.122) | copy-start | bytes 1540
  14.4 236.3 %copy-start.62 = (f32[128]{0:T(128)}, f32[128]{0:T(128)S(1)}, u32[]{:S(2)}) copy-start(f32[128]{0:T(128)S(1)} %add_rsqrt_fusion.1) | copy-start | bytes 1540
  14.4 236.3 %copy-start.64 = (f32[128]{0:T(128)}, f32[128]{0:T(128)S(1)}, u32[]{:S(2)}) copy-start(f32[128]{0:T(128)S(1)} %add_rsqrt_fusion) | copy-start | bytes 1540
  282.2 257.0 %copy-start.13 = (bf16[128,2048]{1,0:T(8,128)(2,1)S(1)}, bf16[128,2048]{1,0:T(8,128)(2,1)}, u32[]{:S(2)}) copy-start(bf16[128,2048]{1,0:T(8,128)(2,1)} %get-tuple-element.49) | copy-start | bytes 1572868
  285.0 271.7 %copy-start.11 = (bf16[128,2048]{1,0:T(8,128)(2,1)S(1)}, bf16[128,2048]{1,0:T(8,128)(2,1)}, u32[]{:S(2)}) copy-start(bf16[128,2048]{1,0:T(8,128)(2,1)} %get-tuple-element.48) | copy-start | bytes 1572868
  539.1 17.6 copy-start.53
  556.7 39.8 %copy-start.24 = (bf16[128,8192]{1,0:T(8,128)(2,1)}, bf16[128,8192]{1,0:T(8,128)(2,1)S(1)}, u32[]{:S(2)}) copy-start(bf16[128,8192]{1,0:T(8,128)(2,1)S(1)} %get-tuple-element.106) | copy-start | bytes 6291460
  556.7 16.7 copy-start.48
  556.8 16.7 copy-start.50
  573.5 23.1 copy-start.22
  602.3 26.3 copy-start.6
  602.3 1178.9 %reduce-scatter.5.cloned.1.call-start = ((), (), s32[]{:S(2)}) async-start(), calls=%async_computation.6 | async-start | bytes 73400320 | tf_op jit(solution)/shard_map/reduce_scatter | solution.py:233
  665.5 261.9 %copy-start.7 = (bf16[2,128,2048]{2,1,0:T(8,128)(2,1)S(1)}, bf16[2,128,2048]{2,1,0:T(8,128)(2,1)}, u32[]{:S(2)}) copy-start(bf16[2,128,2048]{2,1,0:T(8,128)(2,1)} %param.15) | copy-start | bytes 3145732
  1024.1 975.1 %all-reduce.10.cloned.1.call-start = ((), (), s32[]{:S(2)}) async-start(), calls=%async_computation.7 | async-start | bytes 20971520 | tf_op jit(solution)/shard_map/psum | solution.py:274
  1286.7 1692.3 %all-gather.15.cloned.1.call-start = ((), (), s32[]{:S(2)}) async-start(), calls=%async_computation.8 | async-start | bytes 132120576 | tf_op jit(solution)/shard_map/all_gather | solution.py:273
  1825.0 17.5 copy-start.52
  1825.0 17.5 copy-start.57
  1825.0 17.5 copy-start.59
  1825.0 17.5 copy-start.63
  1825.0 17.5 copy-start.65
  1842.5 20.0 copy-start.8
  1842.6 20.0 copy-start.9
  1911.2 1133.1 %copy-start.61 = (f32[512]{0:T(512)}, f32[512]{0:T(512)S(1)}, u32[]{:S(2)}) copy-start(f32[512]{0:T(512)S(1)} %convert_element_type.271) | copy-start | bytes 6148
  1911.8 16.4 copy-start.21
  1911.8 16.4 copy-start.23
  (47 other events, 149.9 us)
Sparse Core Ops, SparseCore 0:
  9.9 230.2 all-gather.6
  242.0 297.0 all-gather.10
  541.0 87.5 all-gather.8
  630.3 297.0 all-gather.12
  930.3 356.2 reduce-scatter.6
  1289.6 491.6 reduce-scatter.4
  1783.6 215.4 all-reduce.9
  2000.8 978.1 all-gather.14
